TPU v7x, 32 devices: a whole 2x2x4 slice. The times are simulated.
32 devices in a mesh: dp: 4 (over y, x), mp: 8 (over z, core).
Axes of the slice: x: 2, y: 2, z: 4, core: 2. Of those that a mesh axis runs over, the one named last changes fastest.
Arguments:
- query_grads: bfloat16 [4, 1, 3584, 4096], P('dp', None, None, 'mp'), may hold values from -102 to 102
- merge_grads: bfloat16 [4, 1, 4096, 3584], P('dp', None, 'mp'), may hold values from -102 to 102
- query_accum: float32 [1, 3584, 4096], P(None, 'dp', 'mp'), may hold values from -406 to 406
- merge_accum: float32 [1, 4096, 3584], P(None, 'mp', 'dp'), may hold values from -406 to 406
- query_master: float32 [1, 3584, 4096], P(None, 'dp', 'mp'), may hold values from -0.75 to 0.75
- merge_master: float32 [1, 4096, 3584], P(None, 'mp', 'dp'), may hold values from -0.75 to 0.75
- query_moment: float32 [1, 3584, 4096], P(None, 'dp', 'mp'), may hold values from -6 to 6
- merge_moment: float32 [1, 4096, 3584], P(None, 'mp', 'dp'), may hold values from -6 to 6
- query_second: float32 [1, 3584, 4096], P(None, 'dp', 'mp'), may hold values from 0.3 to 3
- merge_second: float32 [1, 4096, 3584], P(None, 'mp', 'dp'), may hold values from 0.3 to 3
Outputs:
- query_weight: bfloat16 [1, 3584, 4096], P(None, None, 'mp')
- merge_weight: bfloat16 [1, 4096, 3584], P(None, 'mp')
- query_shard: float32 [1, 3584, 4096], P(None, 'dp', 'mp')
- merge_shard: float32 [1, 4096, 3584], P(None, 'mp', 'dp')
- query_first: float32 [1, 3584, 4096], P(None, 'dp', 'mp')
- merge_first: float32 [1, 4096, 3584], P(None, 'mp', 'dp')
- query_variance: float32 [1, 3584, 4096], P(None, 'dp', 'mp')
- merge_variance: float32 [1, 4096, 3584], P(None, 'mp', 'dp')
All inputs are finite; a program needn't handle non-finite values.
Results may differ from a plain program's by a relative error of at most 0.0015.
Values may be sent and summed in bfloat16 or wider, within the bound.
A program may use at most 128 MiB of HBM per device.

v0:
```python
import functools

import jax
import jax.numpy as jnp
from jax import lax
from jax.experimental import pallas as pl
from jax.experimental.pallas import tpu as pltpu
from jax.sharding import PartitionSpec as P

STEP = 10
ENTRIES = 29360128


beta_one = 0.9
beta_two = 0.95
learn_rate = 0.002
weight_decay = 0.1
adam_eps = 1e-08

CHUNKS = 8
ROWS = 16
MESH_IDS = pl.DeviceIdType.MESH


def adamw(total, clip, master, moment, second):
    scaled = clip * total
    first = beta_one * moment + (1.0 - beta_one) * scaled
    variance = beta_two * second + (1.0 - beta_two) * scaled * scaled
    corr_one = 1.0 - beta_one**STEP
    corr_two = 1.0 - beta_two**STEP
    update = first / corr_one / (jnp.sqrt(variance / corr_two) + adam_eps) + weight_decay * master
    return (master - learn_rate * update, first, variance)


def step_kernel(
    n_mp,
    grads_q, grads_m, accum_q, accum_m, master_q, master_m, moment_q, moment_m, second_q, second_m,
    weight_q, weight_m, shard_q, shard_m, first_q, first_m, variance_q, variance_m,
    near_q, near_m, far_q, far_m, part_q, part_m, came_q, came_m,
    total_q, total_m, mast_q, mast_m, mom_q, mom_m, sec_q, sec_m,
    squares_q, squares_m, tile, tiles,
    local_sem, sum_send, sum_recv, gather_send, gather_recv, tile_send, tile_recv,
):
    me = lax.axis_index("dp")
    mp = lax.axis_index("mp")
    low = me + 1 - 2 * (me % 2)
    high = (me + 2) % 4
    both = 3 - me

    q = dict(
        tag=0, grads=grads_q, one=low, two=high, near=near_q, far=far_q, part=part_q, came=came_q,
        total=total_q, master=mast_q, moment=mom_q, second=sec_q, squares=squares_q,
        weight=weight_q, shard=shard_q, first=first_q, variance=variance_q,
        fetch=((accum_q, total_q), (master_q, mast_q), (moment_q, mom_q), (second_q, sec_q)),
    )
    m = dict(
        tag=1, grads=grads_m, one=high, two=low, near=near_m, far=far_m, part=part_m, came=came_m,
        total=total_m, master=mast_m, moment=mom_m, second=sec_m, squares=squares_m,
        weight=weight_m, shard=shard_m, first=first_m, variance=variance_m,
        fetch=((accum_m, total_m), (master_m, mast_m), (moment_m, mom_m), (second_m, sec_m)),
    )
    sides = (q, m)
    for t in sides:
        t["rows"], t["cols"] = t["total"].shape
        t["step"] = t["rows"] // CHUNKS

    def block(t, ref, owner, start, size):
        if t["tag"] == 0:
            return ref.at[pl.ds(pl.multiple_of(owner * t["rows"] + start, ROWS), size), :]
        return ref.at[
            pl.ds(pl.multiple_of(start, ROWS), size),
            pl.ds(pl.multiple_of(owner * t["cols"], 128), t["cols"]),
        ]

    def chunk(t, c):
        return pl.ds(pl.multiple_of(c * t["step"], ROWS), t["step"])

    def remote(src, dst, send, recv, peer):
        return pltpu.make_async_remote_copy(
            src_ref=src, dst_ref=dst, send_sem=send, recv_sem=recv,
            device_id=(peer, mp), device_id_type=MESH_IDS,
        )

    local = []
    for t in sides:
        pairs = [
            (block(t, t["grads"], t["two"], 0, t["rows"]), t["near"].at[0]),
            (block(t, t["grads"], me, 0, t["rows"]), t["near"].at[1]),
        ] + list(t["fetch"])
        t["local"] = []
        for i, (src, dst) in enumerate(pairs):
            t["local"].append(pltpu.make_async_copy(src, dst, local_sem.at[t["tag"], i]))
        local.append(t["local"])
    for i in range(6):
        for t in sides:
            t["local"][i].start()

    barrier = pltpu.get_barrier_semaphore()
    others = [((me + i) % 4, (mp + k) % n_mp) for i in range(4) for k in range(n_mp) if i + k > 0]
    for peer in others:
        pl.semaphore_signal(barrier, inc=1, device_id=peer, device_id_type=MESH_IDS)
    pl.semaphore_wait(barrier, len(others))

    def first_copy(t, half, c):
        owner = both if half == 0 else t["one"]
        return remote(
            block(t, t["grads"], owner, c * t["step"], t["step"]),
            t["far"].at[half, chunk(t, c)],
            sum_send.at[t["tag"], half, c], sum_recv.at[t["tag"], half, c], t["one"],
        )

    def second_copy(t, c):
        return remote(
            t["part"].at[chunk(t, c)], t["came"].at[chunk(t, c)],
            sum_send.at[t["tag"], 2, c], sum_recv.at[t["tag"], 2, c], t["two"],
        )

    for half in range(2):
        @pl.loop(0, CHUNKS)
        def _(c):
            for t in sides:
                first_copy(t, half, c).start()

    def over_rows(t, c, body):
        @pl.loop(0, t["step"] // ROWS)
        def _(r):
            body(pl.ds(pl.multiple_of(c * t["step"] + r * ROWS, ROWS), ROWS))

    for t in sides:
        t["local"][0].wait()

    @pl.loop(0, CHUNKS)
    def _(c):
        for t in sides:
            first_copy(t, 0, c).wait_recv()

            def add(rows, t=t):
                both_terms = t["near"][0, rows, :].astype(jnp.float32) + t["far"][0, rows, :].astype(jnp.float32)
                t["part"][rows, :] = both_terms.astype(jnp.bfloat16)

            over_rows(t, c, add)
            second_copy(t, c).start()

    for t in sides:
        for i in range(1, 6):
            t["local"][i].wait()
        t["squares"][...] = jnp.zeros_like(t["squares"])

    @pl.loop(0, CHUNKS)
    def _(c):
        for t in sides:
            first_copy(t, 1, c).wait_recv()
            second_copy(t, c).wait_recv()

            def add(rows, t=t):
                own = t["near"][1, rows, :].astype(jnp.float32) + t["far"][1, rows, :].astype(jnp.float32)
                total = t["total"][rows, :] + (own + t["came"][rows, :].astype(jnp.float32))
                t["total"][rows, :] = total
                t["squares"][...] += total * total

            over_rows(t, c, add)

    lanes = tile.shape[1]
    local_squares = jnp.zeros((8, lanes), jnp.float32)
    for t in sides:
        for r in range(ROWS // 8):
            for c in range(t["cols"] // lanes):
                local_squares += t["squares"][r * 8 : (r + 1) * 8, c * lanes : (c + 1) * lanes]
    tile[...] = jnp.sum(local_squares, axis=0, keepdims=True)
    tile_copies = [
        pltpu.make_async_remote_copy(
            src_ref=tile, dst_ref=tiles.at[i], send_sem=tile_send.at[i], recv_sem=tile_recv.at[i],
            device_id=peer, device_id_type=MESH_IDS,
        )
        for i, peer in enumerate(others)
    ]
    for copy in tile_copies:
        copy.start()
    gathered = tile[...]
    for copy in tile_copies:
        copy.wait_recv()
    for i in range(len(others)):
        gathered += tiles[i]
    sumsq = jnp.full(tile.shape, jnp.sum(gathered), jnp.float32)
    clip = jnp.max(jnp.minimum(1.0, lax.rsqrt(sumsq / float(ENTRIES) + 1e-06)))

    def own_copy(t, way, c):
        peer = t["one"] if way == 0 else t["two"]
        ref = block(t, t["weight"], me, c * t["step"], t["step"])
        return remote(
            ref, ref, gather_send.at[t["tag"], way, c], gather_recv.at[t["tag"], way, c], peer
        )

    def passed_copy(t, c):
        ref = block(t, t["weight"], t["two"], c * t["step"], t["step"])
        return remote(
            ref, ref, gather_send.at[t["tag"], 2, c], gather_recv.at[t["tag"], 2, c], t["one"]
        )

    @pl.loop(0, CHUNKS)
    def _(c):
        for t in sides:
            def update(rows, t=t):
                shard, first, variance = adamw(
                    t["total"][rows, :], clip, t["master"][rows, :], t["moment"][rows, :], t["second"][rows, :]
                )
                t["shard"][rows, :] = shard
                t["first"][rows, :] = first
                t["variance"][rows, :] = variance
                if t["tag"] == 0:
                    at = pl.ds(pl.multiple_of(me * t["rows"] + rows.start, ROWS), ROWS)
                    t["weight"][at, :] = shard.astype(jnp.bfloat16)
                else:
                    at = pl.ds(pl.multiple_of(me * t["cols"], 128), t["cols"])
                    t["weight"][rows, at] = shard.astype(jnp.bfloat16)

            over_rows(t, c, update)
            own_copy(t, 1, c).start()
            own_copy(t, 0, c).start()

    @pl.loop(0, CHUNKS)
    def _(c):
        for t in sides:
            own_copy(t, 1, c).wait_recv()
            passed_copy(t, c).start()

    @pl.loop(0, CHUNKS)
    def _(c):
        for t in sides:
            first_copy(t, 0, c).wait_send()
            first_copy(t, 1, c).wait_send()
            second_copy(t, c).wait_send()
            own_copy(t, 0, c).wait()
            own_copy(t, 1, c).wait_send()
            passed_copy(t, c).wait()
    for copy in tile_copies:
        copy.wait_send()


def store_kernel(*refs):
    sem = refs[-1]
    copies = [pltpu.make_async_copy(refs[i], refs[8 + i], sem.at[i]) for i in range(8)]
    for copy in copies:
        copy.start()
    for copy in copies:
        copy.wait()


def square_step(n_mp, *args):
    grads_q, grads_m = args[0][0, 0], args[1][0, 0]
    shards = [a[0] for a in args[2:]]
    shape_q, shape_m = shards[0].shape, shards[1].shape
    f32, bf16 = jnp.float32, jnp.bfloat16
    wide = dict(zip("qm", (shape_q, shape_m)))
    outs = [(grads_q.shape, bf16), (grads_m.shape, bf16)] + [(wide[k], f32) for k in "qmqmqm"]
    scratch = []
    for lead in ((2,), (2,), (), ()):
        scratch += [pltpu.VMEM(lead + wide[k], bf16) for k in "qm"]
    for _ in range(4):
        scratch += [pltpu.VMEM(wide[k], f32) for k in "qm"]
    scratch += [pltpu.VMEM((ROWS, wide[k][1]), f32) for k in "qm"]
    dma = pltpu.SemaphoreType.DMA
    scratch += [
        pltpu.VMEM((1, 128), f32),
        pltpu.VMEM((4 * n_mp - 1, 1, 128), f32),
        dma((2, 6)),
        dma((2, 3, CHUNKS)),
        dma((2, 3, CHUNKS)),
        dma((2, 3, CHUNKS)),
        dma((2, 3, CHUNKS)),
        dma((4 * n_mp - 1,)),
        dma((4 * n_mp - 1,)),
    ]
    results = pl.pallas_call(
        functools.partial(step_kernel, n_mp),
        out_shape=[OUT_SPACE(s, d) for s, d in outs],
        in_specs=[pl.BlockSpec(memory_space=pltpu.HBM)] * 10,
        out_specs=[pl.BlockSpec(memory_space=pltpu.VMEM)] * 8,
        scratch_shapes=scratch,
        compiler_params=pltpu.CompilerParams(
            collective_id=0, has_side_effects=True, vmem_limit_bytes=VMEM_LIMIT
        ),
    )(grads_q, grads_m, *shards)
    stored = pl.pallas_call(
        store_kernel,
        out_shape=[jax.ShapeDtypeStruct(s, d) for s, d in outs],
        in_specs=[pl.BlockSpec(memory_space=pltpu.VMEM)] * 8,
        out_specs=[pl.BlockSpec(memory_space=pltpu.HBM)] * 8,
        scratch_shapes=[dma((8,))],
        compiler_params=pltpu.CompilerParams(vmem_limit_bytes=1024 * 1024),
    )(*[pltpu.with_memory_space_constraint(r, pltpu.VMEM) for r in results])
    return tuple(r[None] for r in stored)


OUT_SPACE = pltpu.VMEM
VMEM_LIMIT = 40 * 1024 * 1024


def on_device(
    query_grads,
    merge_grads,
    query_accum,
    merge_accum,
    query_master,
    merge_master,
    query_moment,
    merge_moment,
    query_second,
    merge_second,
):
    query_sum, merge_sum = (
        lax.psum_scatter(
            query_grads[0].astype(jnp.float32).astype(jnp.bfloat16),
            "dp",
            scatter_dimension=1,
            tiled=True,
        ).astype(jnp.float32),
        lax.psum_scatter(
            merge_grads[0].astype(jnp.float32).astype(jnp.bfloat16),
            "dp",
            scatter_dimension=2,
            tiled=True,
        ).astype(jnp.float32),
    )
    query_total = query_accum + query_sum
    merge_total = merge_accum + merge_sum
    local_squares = jnp.sum(query_total * query_total) + jnp.sum(merge_total * merge_total)
    sumsq = lax.psum(local_squares, ("dp", "mp"))
    clip = jnp.minimum(1.0, lax.rsqrt(sumsq / float(ENTRIES) + 1e-06))
    query_shard, query_first, query_variance = adamw(
        query_total, clip, query_master, query_moment, query_second
    )
    merge_shard, merge_first, merge_variance = adamw(
        merge_total, clip, merge_master, merge_moment, merge_second
    )
    query_weight, merge_weight = (
        lax.all_gather(query_shard.astype(jnp.bfloat16), "dp", axis=1, tiled=True),
        lax.all_gather(merge_shard.astype(jnp.bfloat16), "dp", axis=2, tiled=True),
    )
    return (
        query_weight,
        merge_weight,
        query_shard,
        merge_shard,
        query_first,
        merge_first,
        query_variance,
        merge_variance,
    )


def solution(mesh):
    square = mesh.shape["dp"] == 4
    body = functools.partial(square_step, mesh.shape["mp"]) if square else on_device
    return jax.shard_map(
        body,
        mesh=mesh,
        in_specs=(
            P("dp", None, None, "mp"),
            P("dp", None, "mp", None),
            P(None, "dp", "mp"),
            P(None, "mp", "dp"),
            P(None, "dp", "mp"),
            P(None, "mp", "dp"),
            P(None, "dp", "mp"),
            P(None, "mp", "dp"),
            P(None, "dp", "mp"),
            P(None, "mp", "dp"),
        ),
        out_specs=(
            P(None, None, "mp"),
            P(None, "mp", None),
            P(None, "dp", "mp"),
            P(None, "mp", "dp"),
            P(None, "dp", "mp"),
            P(None, "mp", "dp"),
            P(None, "dp", "mp"),
            P(None, "mp", "dp"),
        ),
        check_vma=False,
    )
```

profile of v0, /device:TPU:0, one launch (start us, length us, event | category | flops | bytes accessed | tf_op | source)
XLA Modules:
  0.0 142.5 jit_solution(17338740056651761485)
XLA Ops:
  0.6 135.4 %shard_map.161 = (bf16[3584,512]{1,0:T(8,128)(2,1)S(1)}, bf16[512,3584]{1,0:T(8,128)(2,1)S(1)}, f32[896,512]{1,0:T(8,128)S(1)}, f32[512,896]{1,0:T(8,128)S(1)}, ...) custom-call(bf16[3584,512]{1,0:T(8,128)(2,1)} %bitcast.18, ...), custom_call_target="tpu_custom_call" | custom-call | tf_op jit(solution)/shard_map/pallas_call | solution.py:274
  136.0 6.5 %shard_map.162 = (bf16[3584,512]{1,0:T(8,128)(2,1)}, bf16[512,3584]{1,0:T(8,128)(2,1)}, f32[896,512]{1,0:T(8,128)}, f32[512,896]{1,0:T(8,128)}, f32[896,512]{1,0...) custom-call(bf16[3584,512]{1,0:T(8,128)(2,1)S(1)} %get-tuple-element.24.refs_0_, ...), custom_call_target="tpu_custom_call" | custom-call | tf_op jit(solution)/shard_map/pallas_call | solution.py:284
where the time goes:
time: 143 us; the launch traced here: 142 us
  Pallas kernels  142 us (99%)
    pallas_call x1, Pallas kernels, square_step(): pl.pallas_call(functools.partial(step_kernel, n_mp), out_shape=[OUT_SPACE...  135 us
    pallas_call x1, Pallas kernels, square_step(): pl.pallas_call(store_kernel, out_shape=[jax.ShapeDtypeStruct(s, d) for s,...  6.48 us

commit v1 on v0

--- a/solution.py
+++ b/solution.py
@@ -19,6 +19,8 @@
 
 CHUNKS = 8
 ROWS = 16
+CORES = 2
+ORDER = (3, 1, 2, 0)
 MESH_IDS = pl.DeviceIdType.MESH
 
 
@@ -39,7 +41,7 @@
     near_q, near_m, far_q, far_m, part_q, part_m, came_q, came_m,
     total_q, total_m, mast_q, mast_m, mom_q, mom_m, sec_q, sec_m,
     squares_q, squares_m, tile, tiles,
-    local_sem, sum_send, sum_recv, gather_send, gather_recv, tile_send, tile_recv,
+    local_sem, send_sem, recv_sem, tile_send, tile_recv, relay_sem,
 ):
     me = lax.axis_index("dp")
     mp = lax.axis_index("mp")
@@ -95,24 +97,43 @@
         for t in sides:
             t["local"][i].start()
 
+    lines, pair = n_mp // CORES, mp % CORES
+    line = mp // CORES
+    near = [(low, mp), (high, mp)]
+    near += [(me, line * CORES + (pair + k) % CORES) for k in range(1, CORES)]
+    up, down = line + 1 < lines, line > 0
+    count = len(near) + up.astype(jnp.int32) + down.astype(jnp.int32)
+
+    def greet(sem):
+        for peer in near:
+            pl.semaphore_signal(sem, inc=1, device_id=peer, device_id_type=MESH_IDS)
+
+        @pl.when(up)
+        def _():
+            pl.semaphore_signal(sem, inc=1, device_id=(me, mp + CORES), device_id_type=MESH_IDS)
+
+        @pl.when(down)
+        def _():
+            pl.semaphore_signal(sem, inc=1, device_id=(me, mp - CORES), device_id_type=MESH_IDS)
+
     barrier = pltpu.get_barrier_semaphore()
-    others = [((me + i) % 4, (mp + k) % n_mp) for i in range(4) for k in range(n_mp) if i + k > 0]
-    for peer in others:
-        pl.semaphore_signal(barrier, inc=1, device_id=peer, device_id_type=MESH_IDS)
-    pl.semaphore_wait(barrier, len(others))
+    greet(barrier)
+    pl.semaphore_wait(barrier, count)
+    hops = relay_sem.shape[0]
+    others = [((me + i) % 4, (mp + k) % n_mp) for i in ORDER for k in range(n_mp) if i + k > 0]
 
     def first_copy(t, half, c):
         owner = both if half == 0 else t["one"]
         return remote(
             block(t, t["grads"], owner, c * t["step"], t["step"]),
             t["far"].at[half, chunk(t, c)],
-            sum_send.at[t["tag"], half, c], sum_recv.at[t["tag"], half, c], t["one"],
+            send_sem.at[t["tag"], half], recv_sem.at[t["tag"], half, c], t["one"],
         )
 
     def second_copy(t, c):
         return remote(
             t["part"].at[chunk(t, c)], t["came"].at[chunk(t, c)],
-            sum_send.at[t["tag"], 2, c], sum_recv.at[t["tag"], 2, c], t["two"],
+            send_sem.at[t["tag"], 2], recv_sem.at[t["tag"], 2, c], t["two"],
         )
 
     for half in range(2):
@@ -125,6 +146,10 @@
         @pl.loop(0, t["step"] // ROWS)
         def _(r):
             body(pl.ds(pl.multiple_of(c * t["step"] + r * ROWS, ROWS), ROWS))
+
+    for i in range(hops):
+        greet(relay_sem.at[i])
+        pl.semaphore_wait(relay_sem.at[i], count)
 
     for t in sides:
         t["local"][0].wait()
@@ -169,7 +194,7 @@
     tile[...] = jnp.sum(local_squares, axis=0, keepdims=True)
     tile_copies = [
         pltpu.make_async_remote_copy(
-            src_ref=tile, dst_ref=tiles.at[i], send_sem=tile_send.at[i], recv_sem=tile_recv.at[i],
+            src_ref=tile, dst_ref=tiles.at[i], send_sem=tile_send, recv_sem=tile_recv,
             device_id=peer, device_id_type=MESH_IDS,
         )
         for i, peer in enumerate(others)
@@ -177,8 +202,7 @@
     for copy in tile_copies:
         copy.start()
     gathered = tile[...]
-    for copy in tile_copies:
-        copy.wait_recv()
+    pltpu.make_async_copy(tiles, tiles, tile_recv).wait()
     for i in range(len(others)):
         gathered += tiles[i]
     sumsq = jnp.full(tile.shape, jnp.sum(gathered), jnp.float32)
@@ -188,13 +212,13 @@
         peer = t["one"] if way == 0 else t["two"]
         ref = block(t, t["weight"], me, c * t["step"], t["step"])
         return remote(
-            ref, ref, gather_send.at[t["tag"], way, c], gather_recv.at[t["tag"], way, c], peer
+            ref, ref, send_sem.at[t["tag"], 3 + way], recv_sem.at[t["tag"], way, c], peer
         )
 
     def passed_copy(t, c):
         ref = block(t, t["weight"], t["two"], c * t["step"], t["step"])
         return remote(
-            ref, ref, gather_send.at[t["tag"], 2, c], gather_recv.at[t["tag"], 2, c], t["one"]
+            ref, ref, send_sem.at[t["tag"], 5], recv_sem.at[t["tag"], 2, c], t["one"]
         )
 
     @pl.loop(0, CHUNKS)
@@ -227,14 +251,14 @@
     @pl.loop(0, CHUNKS)
     def _(c):
         for t in sides:
-            first_copy(t, 0, c).wait_send()
-            first_copy(t, 1, c).wait_send()
-            second_copy(t, c).wait_send()
-            own_copy(t, 0, c).wait()
-            own_copy(t, 1, c).wait_send()
-            passed_copy(t, c).wait()
-    for copy in tile_copies:
-        copy.wait_send()
+            own_copy(t, 0, c).wait_recv()
+            passed_copy(t, c).wait_recv()
+
+    for t in sides:
+        for i in range(6):
+            whole = t["part"]
+            pltpu.make_async_copy(whole, whole, send_sem.at[t["tag"], i]).wait()
+    pltpu.make_async_copy(tiles, tiles, tile_send).wait()
 
 
 def store_kernel(*refs):
@@ -264,12 +288,11 @@
         pltpu.VMEM((1, 128), f32),
         pltpu.VMEM((4 * n_mp - 1, 1, 128), f32),
         dma((2, 6)),
+        dma((2, 6)),
         dma((2, 3, CHUNKS)),
-        dma((2, 3, CHUNKS)),
-        dma((2, 3, CHUNKS)),
-        dma((2, 3, CHUNKS)),
-        dma((4 * n_mp - 1,)),
-        dma((4 * n_mp - 1,)),
+        dma(()),
+        dma(()),
+        pltpu.SemaphoreType.REGULAR((max(n_mp // CORES, 1) + 1,)),
     ]
     results = pl.pallas_call(
         functools.partial(step_kernel, n_mp),
@@ -350,7 +373,7 @@
 
 
 def solution(mesh):
-    square = mesh.shape["dp"] == 4
+    square = mesh.shape["dp"] == 4 and mesh.shape["mp"] % CORES == 0
     body = functools.partial(square_step, mesh.shape["mp"]) if square else on_device
     return jax.shard_map(
         body,

time: 143 us -> 140 us (0.979)
  Pallas kernels: 142 us -> 139 us
    pallas_call x1, Pallas kernels: 135 us -> 132 us  [square_step(): pl.pallas_call(functools.partial(step_kernel, n_mp), out_shape=[OUT_SPACE...]
where the time goes in v1:
time: 140 us; the launch traced here: 139 us
  Pallas kernels  139 us (99%)
    pallas_call x1, Pallas kernels, square_step(): pl.pallas_call(functools.partial(step_kernel, n_mp), out_shape=[OUT_SPACE...  132 us
    pallas_call x1, Pallas kernels, square_step(): pl.pallas_call(store_kernel, out_shape=[jax.ShapeDtypeStruct(s, d) for s,...  6.48 us

profile of v1, /device:TPU:0, one launch (start us, length us, event | category | flops | bytes accessed | tf_op | source)
XLA Modules:
  0.0 139.5 jit_solution(16642955575206804302)
XLA Ops:
  0.6 132.3 %shard_map.161 = (bf16[3584,512]{1,0:T(8,128)(2,1)S(1)}, bf16[512,3584]{1,0:T(8,128)(2,1)S(1)}, f32[896,512]{1,0:T(8,128)S(1)}, f32[512,896]{1,0:T(8,128)S(1)}, ...) custom-call(bf16[3584,512]{1,0:T(8,128)(2,1)} %bitcast.18, ...), custom_call_target="tpu_custom_call" | custom-call | tf_op jit(solution)/shard_map/pallas_call | solution.py:297
  133.0 6.5 %shard_map.162 = (bf16[3584,512]{1,0:T(8,128)(2,1)}, bf16[512,3584]{1,0:T(8,128)(2,1)}, f32[896,512]{1,0:T(8,128)}, f32[512,896]{1,0:T(8,128)}, f32[896,512]{1,0...) custom-call(bf16[3584,512]{1,0:T(8,128)(2,1)S(1)} %get-tuple-element.24.refs_0_, ...), custom_call_target="tpu_custom_call" | custom-call | tf_op jit(solution)/shard_map/pallas_call | solution.py:307

commit v2 on v1

--- a/solution.py
+++ b/solution.py
@@ -20,6 +20,7 @@
 CHUNKS = 8
 ROWS = 16
 CORES = 2
+HELPERS = 2
 ORDER = (3, 1, 2, 0)
 MESH_IDS = pl.DeviceIdType.MESH
 
@@ -40,8 +41,8 @@
     weight_q, weight_m, shard_q, shard_m, first_q, first_m, variance_q, variance_m,
     near_q, near_m, far_q, far_m, part_q, part_m, came_q, came_m,
     total_q, total_m, mast_q, mast_m, mom_q, mom_m, sec_q, sec_m,
-    squares_q, squares_m, tile, tiles,
-    local_sem, send_sem, recv_sem, tile_send, tile_recv, relay_sem,
+    squares_q, squares_m, tile, tiles, early_q, early_m, climb_q, climb_m, cross_q, cross_m,
+    local_sem, send_sem, recv_sem, tile_send, tile_recv, relay_sem, early_sem, climb_sem, cross_sem, hop_sem,
 ):
     me = lax.axis_index("dp")
     mp = lax.axis_index("mp")
@@ -51,13 +52,13 @@
 
     q = dict(
         tag=0, grads=grads_q, one=low, two=high, near=near_q, far=far_q, part=part_q, came=came_q,
-        total=total_q, master=mast_q, moment=mom_q, second=sec_q, squares=squares_q,
+        total=total_q, master=mast_q, moment=mom_q, second=sec_q, squares=squares_q, early=early_q, climb=climb_q, cross=cross_q,
         weight=weight_q, shard=shard_q, first=first_q, variance=variance_q,
         fetch=((accum_q, total_q), (master_q, mast_q), (moment_q, mom_q), (second_q, sec_q)),
     )
     m = dict(
         tag=1, grads=grads_m, one=high, two=low, near=near_m, far=far_m, part=part_m, came=came_m,
-        total=total_m, master=mast_m, moment=mom_m, second=sec_m, squares=squares_m,
+        total=total_m, master=mast_m, moment=mom_m, second=sec_m, squares=squares_m, early=early_m, climb=climb_m, cross=cross_m,
         weight=weight_m, shard=shard_m, first=first_m, variance=variance_m,
         fetch=((accum_m, total_m), (master_m, mast_m), (moment_m, mom_m), (second_m, sec_m)),
     )
@@ -83,7 +84,14 @@
             device_id=(peer, mp), device_id_type=MESH_IDS,
         )
 
-    local = []
+    early = []
+    for t in sides:
+        copy = pltpu.make_async_copy(
+            block(t, t["grads"], both, 0, t["step"]), t["early"], early_sem.at[t["tag"]]
+        )
+        copy.start()
+        early.append(copy)
+
     for t in sides:
         pairs = [
             (block(t, t["grads"], t["two"], 0, t["rows"]), t["near"].at[0]),
@@ -92,10 +100,6 @@
         t["local"] = []
         for i, (src, dst) in enumerate(pairs):
             t["local"].append(pltpu.make_async_copy(src, dst, local_sem.at[t["tag"], i]))
-        local.append(t["local"])
-    for i in range(6):
-        for t in sides:
-            t["local"][i].start()
 
     lines, pair = n_mp // CORES, mp % CORES
     line = mp // CORES
@@ -104,6 +108,9 @@
     up, down = line + 1 < lines, line > 0
     count = len(near) + up.astype(jnp.int32) + down.astype(jnp.int32)
 
+    def at_line(place):
+        return (me, place * CORES + pair)
+
     def greet(sem):
         for peer in near:
             pl.semaphore_signal(sem, inc=1, device_id=peer, device_id_type=MESH_IDS)
@@ -136,11 +143,23 @@
             send_sem.at[t["tag"], 2], recv_sem.at[t["tag"], 2, c], t["two"],
         )
 
+    def early_copy(t):
+        return remote(
+            t["early"], t["far"].at[0, chunk(t, 0)],
+            send_sem.at[t["tag"], 0], recv_sem.at[t["tag"], 0, 0], t["one"],
+        )
+
+    for t in sides:
+        early[t["tag"]].wait()
+        early_copy(t).start()
     for half in range(2):
-        @pl.loop(0, CHUNKS)
+        @pl.loop(1 - half, CHUNKS)
         def _(c):
             for t in sides:
                 first_copy(t, half, c).start()
+    for i in range(6):
+        for t in sides:
+            t["local"][i].start()
 
     def over_rows(t, c, body):
         @pl.loop(0, t["step"] // ROWS)
@@ -219,6 +238,38 @@
         ref = block(t, t["weight"], t["two"], c * t["step"], t["step"])
         return remote(
             ref, ref, send_sem.at[t["tag"], 5], recv_sem.at[t["tag"], 2, c], t["one"]
+        )
+
+    helpers = tuple(range(lines - HELPERS, lines)) if lines > HELPERS + 1 else ()
+
+    def span(t, i):
+        small = t["step"] // HELPERS // ROWS * ROWS
+        return i * small, small if i < HELPERS - 1 else t["step"] - i * small
+
+    def piece(t, ref, owner, i):
+        return block(t, ref, owner, *span(t, i))
+
+    def slot(t, name, i):
+        return t[name].at[pl.ds(0, span(t, i)[1])]
+
+    def climb_copy(t, i, place):
+        return pltpu.make_async_remote_copy(
+            src_ref=piece(t, t["weight"], me, i), dst_ref=slot(t, "climb", i),
+            send_sem=send_sem.at[t["tag"], 3], recv_sem=climb_sem.at[t["tag"]],
+            device_id=at_line(place), device_id_type=MESH_IDS,
+        )
+
+    def cross_copy(t, i):
+        return remote(
+            slot(t, "climb", i), slot(t, "cross", i),
+            hop_sem.at[t["tag"], 0], cross_sem.at[t["tag"]], t["one"],
+        )
+
+    def drop_copy(t, i):
+        return pltpu.make_async_remote_copy(
+            src_ref=slot(t, "cross", i), dst_ref=piece(t, t["weight"], t["one"], i),
+            send_sem=hop_sem.at[t["tag"], 1], recv_sem=recv_sem.at[t["tag"], 0, 0],
+            device_id=at_line(0), device_id_type=MESH_IDS,
         )
 
     @pl.loop(0, CHUNKS)
@@ -240,13 +291,42 @@
 
             over_rows(t, c, update)
             own_copy(t, 1, c).start()
-            own_copy(t, 0, c).start()
+            if not helpers:
+                own_copy(t, 0, c).start()
+            else:
+                around = jnp.logical_and(c == 0, line == 0)
+
+                @pl.when(around)
+                def _():
+                    for i, place in enumerate(helpers):
+                        climb_copy(t, i, place).start()
+
+                @pl.when(jnp.logical_not(around))
+                def _():
+                    own_copy(t, 0, c).start()
+
+    for i, place in enumerate(helpers):
+        @pl.when(line == place)
+        def _():
+            for t in sides:
+                climb_copy(t, i, place).wait_recv()
+                cross_copy(t, i).start()
 
     @pl.loop(0, CHUNKS)
     def _(c):
         for t in sides:
             own_copy(t, 1, c).wait_recv()
             passed_copy(t, c).start()
+
+    for i, place in enumerate(helpers):
+        @pl.when(line == place)
+        def _():
+            for t in sides:
+                cross_copy(t, i).wait_recv()
+                drop_copy(t, i).start()
+            for t in sides:
+                cross_copy(t, i).wait_send()
+                drop_copy(t, i).wait_send()
 
     @pl.loop(0, CHUNKS)
     def _(c):
@@ -287,12 +367,20 @@
     scratch += [
         pltpu.VMEM((1, 128), f32),
         pltpu.VMEM((4 * n_mp - 1, 1, 128), f32),
+    ]
+    for _ in range(3):
+        scratch += [pltpu.VMEM((wide[k][0] // CHUNKS, wide[k][1]), bf16) for k in "qm"]
+    scratch += [
         dma((2, 6)),
         dma((2, 6)),
         dma((2, 3, CHUNKS)),
         dma(()),
         dma(()),
         pltpu.SemaphoreType.REGULAR((max(n_mp // CORES, 1) + 1,)),
+        dma((2,)),
+        dma((2,)),
+        dma((2,)),
+        dma((2, 2)),
     ]
     results = pl.pallas_call(
         functools.partial(step_kernel, n_mp),

time: 140 us -> 137 us (0.979)
  Pallas kernels: 139 us -> 136 us
    pallas_call x1, Pallas kernels: 132 us -> 130 us  [square_step(): pl.pallas_call(functools.partial(step_kernel, n_mp), out_shape=[OUT_SPACE...]
where the time goes in v2:
time: 137 us
  Pallas kernels  136 us (99%)
    pallas_call x1, Pallas kernels, square_step(): pl.pallas_call(functools.partial(step_kernel, n_mp), out_shape=[OUT_SPACE...  130 us
    pallas_call x1, Pallas kernels, square_step(): pl.pallas_call(store_kernel, out_shape=[jax.ShapeDtypeStruct(s, d) for s,...  6.48 us

profile of v2, /device:TPU:0, one launch (start us, length us, event | category | flops | bytes accessed | tf_op | source)
XLA Modules:
  0.0 137.1 jit_solution(17642778940751946523)
XLA Ops:
  0.6 130.0 %shard_map.161 = (bf16[3584,512]{1,0:T(8,128)(2,1)S(1)}, bf16[512,3584]{1,0:T(8,128)(2,1)S(1)}, f32[896,512]{1,0:T(8,128)S(1)}, f32[512,896]{1,0:T(8,128)S(1)}, ...) custom-call(bf16[3584,512]{1,0:T(8,128)(2,1)} %bitcast.18, ...), custom_call_target="tpu_custom_call" | custom-call | tf_op jit(solution)/shard_map/pallas_call | solution.py:385
  130.7 6.5 %shard_map.162 = (bf16[3584,512]{1,0:T(8,128)(2,1)}, bf16[512,3584]{1,0:T(8,128)(2,1)}, f32[896,512]{1,0:T(8,128)}, f32[512,896]{1,0:T(8,128)}, f32[896,512]{1,0...) custom-call(bf16[3584,512]{1,0:T(8,128)(2,1)S(1)} %get-tuple-element.24.refs_0_, ...), custom_call_target="tpu_custom_call" | custom-call | tf_op jit(solution)/shard_map/pallas_call | solution.py:395
